TPU v7x, 512 devices: a whole 4x8x8 slice. The times are simulated.
512 devices in a mesh: gx: 32 (over z, x), gy: 16 (over y, core).
Axes of the slice: x: 4, y: 8, z: 8, core: 2. Of those that a mesh axis runs over, the one named last changes fastest.
Arguments:
- gap_load: float32 [32, 16, 384, 128], P('gx', 'gy'), may hold values from -6 to 6
- flexibility: bfloat16 [32, 16, 768, 768], P('gx', 'gy'), as said below
- schur_blocks: bfloat16 [32, 16, 768, 768], P('gx', 'gy'), as said below
- body_modes: float32 [32, 16, 3, 768], P('gx', 'gy'), may hold values from -6 to 6
- coarse_inverse: float32 [1536, 1536], P(('gx', 'gy')), as said below
- saved_search: float32 [32, 16, 16, 384], P('gx', 'gy'), may hold values from -6 to 6
- saved_images: float32 [32, 16, 16, 384], P('gx', 'gy'), may hold values from -0.0017089844 to 0.0017089844
- face_slots: int32 [32, 16, 4, 192], P('gx', 'gy'), may hold values from 0 to 767, as said below
- face_count: int32 [32, 16, 4], P('gx', 'gy'), may hold values from 0 to 192, as said below
- multiplicity: int32 [32, 16, 768], P('gx', 'gy'), may hold values from 1 to 3, as said below
Outputs:
- multipliers: float32 [32, 16, 384, 128], P('gx', 'gy')
- residual: float32 [32, 16, 384, 128], P('gx', 'gy')
Inputs may be any that keep to these rules, and one draw needn't show every extreme that they name: For k < face_count[a, b, d] the entries face_slots[a, b, d, k] are distinct slots of subdomain (a, b), except that faces that follow each other in the order up, right, down, left share one slot when both are not empty. Link k of the face between two neighbouring subdomains is entry k of both their lists (down of the upper one and up of the lower one, right of the left one and left of the right one). Entries with k >= face_count carry no meaning. face_count[a, b, 0] = face_count[a - 1, b, 1] and face_count[a, b, 2] = face_count[a, b - 1, 3]; faces on the grid's border have 0 links, inner faces between 96 and 192, and in every draw some face along each grid direction has exactly 192. multiplicity[a, b, i] is 1 plus the number of faces of (a, b) whose first face_count entries name slot i. `flexibility`: each block is symmetric. `schur_blocks`: each block is symmetric. `coarse_inverse`: Symmetric.
All inputs are finite; a program needn't handle non-finite values.
Results may differ from a plain program's by a relative error of at most 0.0015.
The roundings to bfloat16 on the way count: a program that leaves them out, or rounds other values in their place, can miss the bound.
Values sent between devices are 32-bit elements.
No kernel may reach another device: no remote copies, remote signals or barrier semaphores. Data moves between devices by JAX's collectives and lax.ppermute only.
A program may use at most 64 MiB of HBM per device.

v0:
```python
import functools
import jax
import jax.numpy as jnp
from jax import lax
from jax.sharding import Mesh
from jax.sharding import PartitionSpec as P

GX = ("gx_0", "gx_1")
GY = ("gy_0", "gy_1")
GX_GY = ("gx_0", "gx_1", "gy_0", "gy_1")
HIGHEST_MODE = lax.Precision.HIGHEST


def shifted(value, axis, steps):
    count = lax.axis_size(axis)
    initial, last = (max(0, -steps), min(count, count - steps))
    return lax.ppermute(value, axis, [(source, source + steps) for source in range(initial, last)])


def over_axes(x, axes):
    return functools.reduce(lax.psum, axes, x)


def place_parts(
    down_values, right_values, from_above, from_left, slot_table, face_valid, slot_total
):
    load_cases = down_values.shape[1]
    signed_parts = (
        jnp.stack([-from_above, down_values, -from_left, right_values], axis=0)
        * face_valid[:, :, None]
    )
    empty = jnp.zeros((slot_total, load_cases), jnp.float32)
    return empty.at[slot_table.reshape(-1)].add(signed_parts.reshape(-1, load_cases))


def place_full(full_links, slot_table, face_valid, slot_total):
    return place_parts(
        full_links[1],
        full_links[3],
        full_links[0],
        full_links[2],
        slot_table,
        face_valid,
        slot_total,
    )


def gain_copies(link_values, face_width):
    down_values = link_values[:face_width]
    right_values = link_values[face_width:]
    upper_copy = shifted(down_values, GX, 1)
    left_copy = shifted(right_values, GY, 1)
    return jnp.stack([upper_copy, down_values, left_copy, right_values], axis=0)


def own_links(full_links):
    return jnp.concatenate([full_links[1], full_links[3]], axis=0)


def jumps_full(slot_values, slot_table, face_valid):
    face_width = slot_table.shape[1]
    picked = jnp.take(slot_values, slot_table.reshape(-1), axis=0).reshape(
        4, face_width, slot_values.shape[1]
    )
    below_values = shifted(picked[0], GX, -1)
    right_values = shifted(picked[2], GY, -1)
    above_values = shifted(picked[1], GX, 1)
    left_values = shifted(picked[3], GY, 1)
    down_part = (picked[1] - below_values) * face_valid[1][:, None]
    right_part = (picked[3] - right_values) * face_valid[3][:, None]
    upper_part = (above_values - picked[0]) * face_valid[0][:, None]
    left_part = (left_values - picked[2]) * face_valid[2][:, None]
    return jnp.stack([upper_part, down_part, left_part, right_part], axis=0)


def late_dots(energy_part, intersect_part):
    return (over_axes(energy_part, GX_GY), over_axes(intersect_part, GX_GY))


def curvature_sum(curvature_part):
    return over_axes(curvature_part, GX_GY)


def per_device(
    gap_load,
    flexibility,
    schur_blocks,
    body_modes,
    coarse_inverse,
    saved_search,
    saved_images,
    face_slots,
    face_count,
    multiplicity,
):
    local_flex = flexibility[0, 0]
    local_schur = schur_blocks[0, 0]
    rigid_modes = body_modes[0, 0]
    slot_table = face_slots[0, 0]
    face_width = slot_table.shape[1]
    slot_total = rigid_modes.shape[1]
    face_valid = (jnp.arange(face_width)[None, :] < face_count[0, 0][:, None]).astype(jnp.float32)
    link_valid = jnp.concatenate([face_valid[1], face_valid[3]], axis=0)
    weights = 1.0 / multiplicity[0, 0].astype(jnp.float32)
    residual = gap_load[0, 0] * link_valid[:, None]
    kept_search = saved_search[0, 0] * link_valid[None, :]
    kept_images = saved_images[0, 0] * link_valid[None, :]
    residual_full = gain_copies(residual, face_width)
    search_full_kept = gain_copies(kept_search.T, face_width)
    weighted = (
        weights[:, None] * place_full(residual_full, slot_table, face_valid, slot_total)
    ).astype(jnp.bfloat16)
    smoothed = jnp.dot(local_schur, weighted, preferred_element_type=jnp.float32)
    precond_full = jumps_full(weights[:, None] * smoothed, slot_table, face_valid)
    precond = own_links(precond_full)
    energy_part = jnp.sum(own_links(residual_full) * precond, axis=0)
    coarse_in = jnp.dot(
        rigid_modes,
        place_full(precond_full, slot_table, face_valid, slot_total),
        precision=HIGHEST_MODE,
    )
    coarse_out = jnp.dot(
        coarse_inverse, lax.all_gather(coarse_in, GX_GY, axis=0, tiled=True), precision=HIGHEST_MODE
    )
    projected_full = precond_full - jumps_full(
        jnp.dot(rigid_modes.T, coarse_out, precision=HIGHEST_MODE), slot_table, face_valid
    )
    intersect_part = jnp.dot(kept_images, own_links(projected_full), precision=HIGHEST_MODE)
    energy, intersect = late_dots(energy_part, intersect_part)
    search_full = projected_full - jnp.einsum(
        "dfj,jc->dfc", search_full_kept, intersect, precision=HIGHEST_MODE
    )
    lifted = place_full(search_full, slot_table, face_valid, slot_total).astype(jnp.bfloat16)
    applied_full = jumps_full(
        jnp.dot(local_flex, lifted, preferred_element_type=jnp.float32), slot_table, face_valid
    )
    search = own_links(search_full)
    curvature = curvature_sum(jnp.sum(search * own_links(applied_full), axis=0))
    step_size = energy / curvature
    multipliers = step_size * search
    residual_full = residual_full - step_size * applied_full
    residual = own_links(residual_full)
    return (multipliers[None, None], residual[None, None])


def solution(mesh):
    split = Mesh(mesh.devices.reshape(8, 4, 8, 2), ("gx_0", "gx_1", "gy_0", "gy_1"))
    placed = (
        P(GX, GY, None, None),
        P(GX, GY, None, None),
        P(GX, GY, None, None),
        P(GX, GY, None, None),
        P(GX_GY, None),
        P(GX, GY, None, None),
        P(GX, GY, None, None),
        P(GX, GY, None, None),
        P(GX, GY, None),
        P(GX, GY, None),
    )
    return jax.shard_map(
        per_device,
        mesh=split,
        in_specs=placed,
        out_specs=(P(GX, GY, None, None), P(GX, GY, None, None)),
        check_vma=False,
    )
```

profile of v0, /device:TPU:1, one launch (start us, length us, event | category | flops | bytes accessed | tf_op | source)
XLA Modules:
  0.0 272.1 jit_solution(19171111291158714)
XLA Ops:
  2.7 4.6 %collective-permute-start.1 = (f32[192,128]{1,0:T(8,128)S(1)}, f32[192,128]{1,0:T(8,128)S(1)}, u32[]{:S(2)}, u32[]{:S(2)}) collective-permute-start(f32[192,128]{1,0:T(8,128)S(1)} %get-tuple-element.54), channel_id=1, source_target_pairs={{0,1},{1,2},{2,3},{3,4},{4,5},{5,6},{6,7},{7,8},{8,9},{9,10},{10,1... | collective-permute-start | bytes 294920 | tf_op jit(solution)/shard_map/ppermute | solution.py:17
  7.3 3.1 %collective-permute-start = (f32[192,128]{1,0:T(8,128)S(1)}, f32[192,128]{1,0:T(8,128)S(1)}, u32[]{:S(2)}, u32[]{:S(2)}) collective-permute-start(f32[192,128]{1,0:T(8,128)S(1)} %get-tuple-element.51), channel_id=1, source_target_pairs={{0,16},{16,32},{32,48},{48,64},{64,80},{80,96},{96,112},{112,128},... | collective-permute-start | bytes 294920 | tf_op jit(solution)/shard_map/ppermute | solution.py:17
  13.6 6.6 %scatter_custom_fusion = f32[768,128]{1,0:T(8,128)S(1)} fusion(s32[768]{0:T(1024)S(1)} %fusion.40, f32[768,128]{1,0:T(8,128)S(1)} %bitcast_multiply_fusion.2, f32[]{:T(128)} %constant.2.clone.1), kind=kCustom, calls=%fused_computation.53 | custom fusion | flops 98304 | bytes 393220 | tf_op jit(solution)/shard_map/scatter-add | solution.py:33
  22.9 3.0 %collective-permute-start.4 = (f32[192,128]{1,0:T(8,128)S(1)}, f32[192,128]{1,0:T(8,128)S(1)}, u32[]{:S(2)}, u32[]{:S(2)}) collective-permute-start(f32[192,128]{1,0:T(8,128)S(1)} %get-tuple-element.47), channel_id=1, source_target_pairs={{0,16},{16,32},{32,48},{48,64},{64,80},{80,96},{96,112},{112,128},... | collective-permute-start | bytes 294920 | tf_op jit(solution)/shard_map/ppermute | solution.py:17
  25.9 3.4 %collective-permute-start.5 = (f32[192,128]{1,0:T(8,128)S(1)}, f32[192,128]{1,0:T(8,128)S(1)}, u32[]{:S(2)}, u32[]{:S(2)}) collective-permute-start(f32[192,128]{1,0:T(8,128)S(1)} %get-tuple-element.49), channel_id=1, source_target_pairs={{0,1},{1,2},{2,3},{3,4},{4,5},{5,6},{6,7},{7,8},{8,9},{9,10},{10,1... | collective-permute-start | bytes 294920 | tf_op jit(solution)/shard_map/ppermute | solution.py:17
  30.6 2.5 collective-permute-start.3
  37.6 6.6 %scatter_custom_fusion.1 = f32[768,128]{1,0:T(8,128)S(1)} fusion(s32[768]{0:T(1024)S(1)} %fusion.40, f32[768,128]{1,0:T(8,128)S(1)} %bitcast_multiply_fusion.1, f32[]{:T(128)} %constant.2.clone.1), kind=kCustom, calls=%fused_computation.51 | custom fusion | flops 98304 | bytes 393220 | tf_op jit(solution)/shard_map/scatter-add | solution.py:33
  44.5 85.6 %all-gather = f32[512,3,128]{2,1,0:T(4,128)S(1)} all-gather(f32[1,3,128]{2,1,0:T(4,128)S(1)} %convolution_bitcast_fusion.2), channel_id=1, replica_groups=mesh['gx_0'=8,'gx_1'=4,'gy_0'=8,'gy_1'=2] {'gx_0','gx_1','gy_0','gy_1'}, dimensions={0}, use_global_device_ids=true | all-gather | bytes 787968 | tf_op jit(solution)/shard_map/all_gather | solution.py:123
  134.4 2.8 %collective-permute-start.6 = (f32[192,128]{1,0:T(8,128)S(1)}, f32[192,128]{1,0:T(8,128)S(1)}, u32[]{:S(2)}, u32[]{:S(2)}) collective-permute-start(f32[192,128]{1,0:T(8,128)S(1)} %get-tuple-element.39), channel_id=1, source_target_pairs={{0,16},{16,32},{32,48},{48,64},{64,80},{80,96},{96,112},{112,128},... | collective-permute-start | bytes 294920 | tf_op jit(solution)/shard_map/ppermute | solution.py:17
  138.5 2.3 collective-permute-start.9
  140.8 3.2 %collective-permute-start.8 = (f32[192,128]{1,0:T(8,128)S(1)}, f32[192,128]{1,0:T(8,128)S(1)}, u32[]{:S(2)}, u32[]{:S(2)}) collective-permute-start(f32[192,128]{1,0:T(8,128)S(1)} %get-tuple-element.41), channel_id=1, source_target_pairs={{0,1},{1,2},{2,3},{3,4},{4,5},{5,6},{6,7},{7,8},{8,9},{9,10},{10,1... | collective-permute-start | bytes 294920 | tf_op jit(solution)/shard_map/ppermute | solution.py:17
  144.1 1.9 collective-permute-start.11
  146.1 4.0 %collective-permute-start.10 = (f32[192,16]{0,1:T(8,128)S(1)}, f32[192,16]{0,1:T(8,128)S(1)}, u32[]{:S(2)}, u32[]{:S(2)}) collective-permute-start(f32[192,16]{0,1:T(8,128)S(1)} %get-tuple-element.55), channel_id=1, source_target_pairs={{0,16},{16,32},{32,48},{48,64},{64,80},{80,96},{96,112},{112,128},... | collective-permute-start | bytes 36872 | tf_op jit(solution)/shard_map/ppermute | solution.py:17
  150.7 14.6 %psum.88 = f32[16,128]{1,0:T(8,128)S(1)} all-reduce(f32[16,128]{1,0:T(8,128)S(1)} %fusion.10), channel_id=1, replica_groups=mesh['gx_0'=8,'gx_1'=4,'gy_0'=8,'gy_1'=2] {'gx_0'}, use_global_device_ids=true, to_apply=%region_7.9 | all-reduce | flops 2048 | bytes 16384 | tf_op jit(solution)/shard_map/psum | solution.py:21
  165.2 10.0 %psum.89 = f32[16,128]{1,0:T(8,128)S(1)} all-reduce(f32[16,128]{1,0:T(8,128)S(1)} %psum.88), channel_id=1, replica_groups=mesh['gx_0'=8,'gx_1'=4,'gy_0'=8,'gy_1'=2] {'gx_1'}, use_global_device_ids=true, to_apply=%region_8.10 | all-reduce | flops 2048 | bytes 16384 | tf_op jit(solution)/shard_map/psum | solution.py:21
  175.2 13.5 %psum.90 = f32[16,128]{1,0:T(8,128)S(1)} all-reduce(f32[16,128]{1,0:T(8,128)S(1)} %psum.89), channel_id=1, replica_groups=mesh['gx_0'=8,'gx_1'=4,'gy_0'=8,'gy_1'=2] {'gy_0'}, use_global_device_ids=true, to_apply=%region_9.11 | all-reduce | flops 2048 | bytes 16384 | tf_op jit(solution)/shard_map/psum | solution.py:21
  188.7 11.6 %psum.91 = f32[16,128]{1,0:T(8,128)S(1)} all-reduce(f32[16,128]{1,0:T(8,128)S(1)} %psum.90), channel_id=1, replica_groups=mesh['gx_0'=8,'gx_1'=4,'gy_0'=8,'gy_1'=2] {'gy_1'}, use_global_device_ids=true, to_apply=%region_10.12 | all-reduce | flops 2048 | bytes 16384 | tf_op jit(solution)/shard_map/psum | solution.py:21
  202.1 6.9 %scatter_custom_fusion.2 = f32[768,128]{1,0:T(8,128)S(1)} fusion(s32[768]{0:T(1024)} %copy-done.31, f32[768,128]{1,0:T(8,128)S(1)} %bitcast_multiply_fusion, f32[]{:T(128)} %constant.2.clone.1), kind=kCustom, calls=%fused_computation.49 | custom fusion | flops 98304 | bytes 393728 | tf_op jit(solution)/shard_map/scatter-add | solution.py:33
  214.3 2.4 collective-permute-start.13
  216.8 3.1 %collective-permute-start.15 = (f32[192,128]{1,0:T(8,128)S(1)}, f32[192,128]{1,0:T(8,128)S(1)}, u32[]{:S(2)}, u32[]{:S(2)}) collective-permute-start(f32[192,128]{1,0:T(8,128)S(1)} %get-tuple-element.23), channel_id=1, source_target_pairs={{0,1},{1,2},{2,3},{3,4},{4,5},{5,6},{6,7},{7,8},{8,9},{9,10},{10,1... | collective-permute-start | bytes 294920 | tf_op jit(solution)/shard_map/ppermute | solution.py:17
  221.8 16.6 %all-reduce.1 = (f32[128]{0:T(128)S(1)}, f32[128]{0:T(128)S(1)}) all-reduce(f32[128]{0:T(128)S(1)} %fusion.9, f32[128]{0:T(128)S(1)} %fusion.14), channel_id=1, replica_groups=mesh['gx_0'=8,'gx_1'=4,'gy_0'=8,'gy_1'=2] {'gx_0'}, use_global_device_ids=true, to_apply=%region_2.4 | all-reduce | flops 256 | bytes 2048 | tf_op jit(solution)/shard_map/psum | solution.py:21
  238.5 6.3 %all-reduce.2 = (f32[128]{0:T(128)S(1)}, f32[128]{0:T(128)S(1)}) all-reduce(f32[128]{0:T(128)S(1)} %get-tuple-element.5, f32[128]{0:T(128)S(1)} %get-tuple-element.6), channel_id=1, replica_groups=mesh['gx_0'=8,'gx_1'=4,'gy_0'=8,'gy_1'=2] {'gx_1'}, use_global_device_ids=true, to_apply=%region_3.5 | all-reduce | flops 256 | bytes 2048 | tf_op jit(solution)/shard_map/psum | solution.py:21
  244.7 12.4 %all-reduce = (f32[128]{0:T(128)S(1)}, f32[128]{0:T(128)S(1)}) all-reduce(f32[128]{0:T(128)S(1)} %get-tuple-element.7, f32[128]{0:T(128)S(1)} %get-tuple-element.8), channel_id=1, replica_groups=mesh['gx_0'=8,'gx_1'=4,'gy_0'=8,'gy_1'=2] {'gy_0'}, use_global_device_ids=true, to_apply=%region_4.6 | all-reduce | flops 256 | bytes 2048 | tf_op jit(solution)/shard_map/psum | solution.py:21
  257.1 13.5 %all-reduce.3 = (f32[128]{0:T(128)S(1)}, f32[128]{0:T(128)S(1)}) all-reduce(f32[128]{0:T(128)S(1)} %get-tuple-element.3, f32[128]{0:T(128)S(1)} %get-tuple-element.4), channel_id=1, replica_groups=mesh['gx_0'=8,'gx_1'=4,'gy_0'=8,'gy_1'=2] {'gy_1'}, use_global_device_ids=true, to_apply=%region_5.7 | all-reduce | flops 256 | bytes 2048 | tf_op jit(solution)/shard_map/psum | solution.py:21
  (140 shorter events, 30.0 us)
Async XLA Ops:
  1.5 35.1 %copy-start.17 = (f32[1,192]{1,0:T(1,128)}, f32[1,192]{1,0:T(1,128)S(1)}, u32[]{:S(2)}) copy-start(f32[1,192]{1,0:T(1,128)S(1)} %get-tuple-element.61) | copy-start | bytes 2308
  1.5 35.1 %copy-start.19 = (f32[1,192]{1,0:T(1,128)}, f32[1,192]{1,0:T(1,128)S(1)}, u32[]{:S(2)}) copy-start(f32[1,192]{1,0:T(1,128)S(1)} %get-tuple-element.62) | copy-start | bytes 2308
  1.6 148.8 %copy-start.15 = (f32[384]{0:T(512)}, f32[384]{0:T(512)S(1)}, u32[]{:S(2)}) copy-start(f32[384]{0:T(512)S(1)} %pad_maximum_fusion.9) | copy-start | bytes 4612
  2.7 10.1 %collective-permute-start.1 = (f32[192,128]{1,0:T(8,128)S(1)}, f32[192,128]{1,0:T(8,128)S(1)}, u32[]{:S(2)}, u32[]{:S(2)}) collective-permute-start(f32[192,128]{1,0:T(8,128)S(1)} %get-tuple-element.54), channel_id=1, source_target_pairs={{0,1},{1,2},{2,3},{3,4},{4,5},{5,6},{6,7},{7,8},{8,9},{9,10},{10,1... | collective-permute-start | bytes 294920 | tf_op jit(solution)/shard_map/ppermute | solution.py:17
  7.3 5.6 %collective-permute-start = (f32[192,128]{1,0:T(8,128)S(1)}, f32[192,128]{1,0:T(8,128)S(1)}, u32[]{:S(2)}, u32[]{:S(2)}) collective-permute-start(f32[192,128]{1,0:T(8,128)S(1)} %get-tuple-element.51), channel_id=1, source_target_pairs={{0,16},{16,32},{32,48},{48,64},{64,80},{80,96},{96,112},{112,128},... | collective-permute-start | bytes 294920 | tf_op jit(solution)/shard_map/ppermute | solution.py:17
  12.8 119.7 %copy-start.13 = (s32[1024]{0:T(1024)}, s32[1024]{0:T(1024)S(1)}, u32[]{:S(2)}) copy-start(s32[1024]{0:T(1024)S(1)} %pad_clamp_fusion) | copy-start | bytes 12292
  22.9 10.3 %collective-permute-start.4 = (f32[192,128]{1,0:T(8,128)S(1)}, f32[192,128]{1,0:T(8,128)S(1)}, u32[]{:S(2)}, u32[]{:S(2)}) collective-permute-start(f32[192,128]{1,0:T(8,128)S(1)} %get-tuple-element.47), channel_id=1, source_target_pairs={{0,16},{16,32},{32,48},{48,64},{64,80},{80,96},{96,112},{112,128},... | collective-permute-start | bytes 294920 | tf_op jit(solution)/shard_map/ppermute | solution.py:17
  25.9 7.3 %collective-permute-start.5 = (f32[192,128]{1,0:T(8,128)S(1)}, f32[192,128]{1,0:T(8,128)S(1)}, u32[]{:S(2)}, u32[]{:S(2)}) collective-permute-start(f32[192,128]{1,0:T(8,128)S(1)} %get-tuple-element.49), channel_id=1, source_target_pairs={{0,1},{1,2},{2,3},{3,4},{4,5},{5,6},{6,7},{7,8},{8,9},{9,10},{10,1... | collective-permute-start | bytes 294920 | tf_op jit(solution)/shard_map/ppermute | solution.py:17
  29.3 5.4 %collective-permute-start.2 = (f32[192,128]{1,0:T(8,128)S(1)}, f32[192,128]{1,0:T(8,128)S(1)}, u32[]{:S(2)}, u32[]{:S(2)}) collective-permute-start(f32[192,128]{1,0:T(8,128)S(1)} %get-tuple-element.50), channel_id=1, source_target_pairs={{16,0},{32,16},{48,32},{64,48},{80,64},{96,80},{112,96},{128,112},... | collective-permute-start | bytes 294920 | tf_op jit(solution)/shard_map/ppermute | solution.py:17
  30.6 5.9 %collective-permute-start.3 = (f32[192,128]{1,0:T(8,128)S(1)}, f32[192,128]{1,0:T(8,128)S(1)}, u32[]{:S(2)}, u32[]{:S(2)}) collective-permute-start(f32[192,128]{1,0:T(8,128)S(1)} %get-tuple-element.48), channel_id=1, source_target_pairs={{1,0},{2,1},{3,2},{4,3},{5,4},{6,5},{7,6},{8,7},{9,8},{10,9},{11,1... | collective-permute-start | bytes 294920 | tf_op jit(solution)/shard_map/ppermute | solution.py:17
  134.4 11.7 %collective-permute-start.6 = (f32[192,128]{1,0:T(8,128)S(1)}, f32[192,128]{1,0:T(8,128)S(1)}, u32[]{:S(2)}, u32[]{:S(2)}) collective-permute-start(f32[192,128]{1,0:T(8,128)S(1)} %get-tuple-element.39), channel_id=1, source_target_pairs={{0,16},{16,32},{32,48},{48,64},{64,80},{80,96},{96,112},{112,128},... | collective-permute-start | bytes 294920 | tf_op jit(solution)/shard_map/ppermute | solution.py:17
  137.2 12.9 %collective-permute-start.7 = (f32[192,128]{1,0:T(8,128)S(1)}, f32[192,128]{1,0:T(8,128)S(1)}, u32[]{:S(2)}, u32[]{:S(2)}) collective-permute-start(f32[192,128]{1,0:T(8,128)S(1)} %get-tuple-element.42), channel_id=1, source_target_pairs={{16,0},{32,16},{48,32},{64,48},{80,64},{96,80},{112,96},{128,112},... | collective-permute-start | bytes 294920 | tf_op jit(solution)/shard_map/ppermute | solution.py:17
  138.5 11.6 %collective-permute-start.9 = (f32[192,128]{1,0:T(8,128)S(1)}, f32[192,128]{1,0:T(8,128)S(1)}, u32[]{:S(2)}, u32[]{:S(2)}) collective-permute-start(f32[192,128]{1,0:T(8,128)S(1)} %get-tuple-element.40), channel_id=1, source_target_pairs={{1,0},{2,1},{3,2},{4,3},{5,4},{6,5},{7,6},{8,7},{9,8},{10,9},{11,1... | collective-permute-start | bytes 294920 | tf_op jit(solution)/shard_map/ppermute | solution.py:17
  140.8 9.3 %collective-permute-start.8 = (f32[192,128]{1,0:T(8,128)S(1)}, f32[192,128]{1,0:T(8,128)S(1)}, u32[]{:S(2)}, u32[]{:S(2)}) collective-permute-start(f32[192,128]{1,0:T(8,128)S(1)} %get-tuple-element.41), channel_id=1, source_target_pairs={{0,1},{1,2},{2,3},{3,4},{4,5},{5,6},{6,7},{7,8},{8,9},{9,10},{10,1... | collective-permute-start | bytes 294920 | tf_op jit(solution)/shard_map/ppermute | solution.py:17
  144.1 56.2 %collective-permute-start.11 = (f32[192,16]{0,1:T(8,128)S(1)}, f32[192,16]{0,1:T(8,128)S(1)}, u32[]{:S(2)}, u32[]{:S(2)}) collective-permute-start(f32[192,16]{0,1:T(8,128)S(1)} %get-tuple-element.58), channel_id=1, source_target_pairs={{0,1},{1,2},{2,3},{3,4},{4,5},{5,6},{6,7},{7,8},{8,9},{9,10},{10,1... | collective-permute-start | bytes 36872 | tf_op jit(solution)/shard_map/ppermute | solution.py:17
  146.1 54.2 %collective-permute-start.10 = (f32[192,16]{0,1:T(8,128)S(1)}, f32[192,16]{0,1:T(8,128)S(1)}, u32[]{:S(2)}, u32[]{:S(2)}) collective-permute-start(f32[192,16]{0,1:T(8,128)S(1)} %get-tuple-element.55), channel_id=1, source_target_pairs={{0,16},{16,32},{32,48},{48,64},{64,80},{80,96},{96,112},{112,128},... | collective-permute-start | bytes 36872 | tf_op jit(solution)/shard_map/ppermute | solution.py:17
  211.6 59.0 %copy-start.4 = (f32[192,128]{1,0:T(8,128)S(1)}, f32[192,128]{1,0:T(8,128)}, u32[]{:S(2)}) copy-start(f32[192,128]{1,0:T(8,128)} %copy-done.3) | copy-start | bytes 294916
  211.6 59.0 %copy-start.6 = (f32[192,128]{1,0:T(8,128)S(1)}, f32[192,128]{1,0:T(8,128)}, u32[]{:S(2)}) copy-start(f32[192,128]{1,0:T(8,128)} %copy-done.5) | copy-start | bytes 294916
  211.6 8.5 %collective-permute-start.14 = (f32[192,128]{1,0:T(8,128)S(1)}, f32[192,128]{1,0:T(8,128)S(1)}, u32[]{:S(2)}, u32[]{:S(2)}) collective-permute-start(f32[192,128]{1,0:T(8,128)S(1)} %get-tuple-element.21), channel_id=1, source_target_pairs={{0,16},{16,32},{32,48},{48,64},{64,80},{80,96},{96,112},{112,128},... | collective-permute-start | bytes 294920 | tf_op jit(solution)/shard_map/ppermute | solution.py:17
  213.0 7.0 %collective-permute-start.12 = (f32[192,128]{1,0:T(8,128)S(1)}, f32[192,128]{1,0:T(8,128)S(1)}, u32[]{:S(2)}, u32[]{:S(2)}) collective-permute-start(f32[192,128]{1,0:T(8,128)S(1)} %get-tuple-element.24), channel_id=1, source_target_pairs={{16,0},{32,16},{48,32},{64,48},{80,64},{96,80},{112,96},{128,112},... | collective-permute-start | bytes 294920 | tf_op jit(solution)/shard_map/ppermute | solution.py:17
  214.3 5.9 %collective-permute-start.13 = (f32[192,128]{1,0:T(8,128)S(1)}, f32[192,128]{1,0:T(8,128)S(1)}, u32[]{:S(2)}, u32[]{:S(2)}) collective-permute-start(f32[192,128]{1,0:T(8,128)S(1)} %get-tuple-element.22), channel_id=1, source_target_pairs={{1,0},{2,1},{3,2},{4,3},{5,4},{6,5},{7,6},{8,7},{9,8},{10,9},{11,1... | collective-permute-start | bytes 294920 | tf_op jit(solution)/shard_map/ppermute | solution.py:17
  216.8 4.7 %collective-permute-start.15 = (f32[192,128]{1,0:T(8,128)S(1)}, f32[192,128]{1,0:T(8,128)S(1)}, u32[]{:S(2)}, u32[]{:S(2)}) collective-permute-start(f32[192,128]{1,0:T(8,128)S(1)} %get-tuple-element.23), channel_id=1, source_target_pairs={{0,1},{1,2},{2,3},{3,4},{4,5},{5,6},{6,7},{7,8},{8,9},{9,10},{10,1... | collective-permute-start | bytes 294920 | tf_op jit(solution)/shard_map/ppermute | solution.py:17
  221.7 49.0 %copy-start.7 = (f32[1,1,192,128]{3,2,1,0:T(8,128)S(1)}, f32[1,1,192,128]{3,2,1,0:T(8,128)}, u32[]{:S(2)}) copy-start(f32[1,1,192,128]{3,2,1,0:T(8,128)} %get-tuple-element.27) | copy-start | bytes 294916
  221.7 49.0 %copy-start.8 = (f32[1,1,192,128]{3,2,1,0:T(8,128)S(1)}, f32[1,1,192,128]{3,2,1,0:T(8,128)}, u32[]{:S(2)}) copy-start(f32[1,1,192,128]{3,2,1,0:T(8,128)} %get-tuple-element.29) | copy-start | bytes 294916
  (24 other events, 296.4 us)
where the time goes:
time: 273 us; the launch traced here: 272 us
  blocking collectives  184 us (67%)
  starting transfers between devices  41.7 us (15%)
  other arithmetic  27.5 us (10%)
  local copies, waits for them, and re-layouts  8.11 us (3%)
  waiting for transfers between devices  4.85 us (2%)
  matrix products  4.32 us (2%)
    psum x8, blocking collectives, over_axes(): return functools.reduce(lax.psum, axes, x)  98.4 us
    all_gather x1, blocking collectives, per_device(): lax.all_gather(coarse_in, GX_GY, axis=0, tiled=True)  85.6 us
    ppermute x16, starting transfers between devices, shifted(): lax.ppermute(value, axis, [(source, source + steps) for source in range(i...  41.7 us
    scatter-add x3, other arithmetic, place_parts(): empty.at[slot_table.reshape(-1)].add(signed_parts.reshape(-1, load_cases))  20.1 us
  transfers between devices with their start and end apart: 16, of which 4 were waited for; matrix products, arithmetic and copies ran while one was open for 1% of the time, Pallas kernels for 0%

commit v1 on v0

--- a/solution.py
+++ b/solution.py
@@ -120,7 +120,17 @@
         precision=HIGHEST_MODE,
     )
     coarse_out = jnp.dot(
-        coarse_inverse, lax.all_gather(coarse_in, GX_GY, axis=0, tiled=True), precision=HIGHEST_MODE
+        coarse_inverse,
+        jnp.concatenate(
+            lax.all_to_all(
+                jnp.stack([coarse_in] * lax.axis_size(GX_GY), axis=0),
+                GX_GY,
+                split_axis=0,
+                concat_axis=0,
+            ),
+            0,
+        ),
+        precision=HIGHEST_MODE,
     )
     projected_full = precond_full - jumps_full(
         jnp.dot(rigid_modes.T, coarse_out, precision=HIGHEST_MODE), slot_table, face_valid

time: 273 us -> 245 us (0.90)
  blocking collectives: 184 us -> 94.9 us
  waiting for transfers between devices: 4.85 us -> 38.5 us
  starting transfers between devices: 41.7 us -> 67.1 us
    all_gather x1 -> x0, blocking collectives: 85.6 us -> none  [per_device(): lax.all_gather(coarse_in, GX_GY, axis=0, tiled=True)]
    all_to_all x0 -> x1, waiting for transfers between devices: none -> 33.6 us  [per_device(): lax.all_to_all(jnp.stack([coarse_in] * lax.axis_size(GX_GY), axis=0), GX_...]
    all_to_all x0 -> x1, starting transfers between devices: none -> 26.1 us  [per_device(): lax.all_to_all(jnp.stack([coarse_in] * lax.axis_size(GX_GY), axis=0), GX_...]
    psum x8, blocking collectives: 98.4 us -> 94.9 us  [over_axes(): return functools.reduce(lax.psum, axes, x)]
  transfers between devices with their start and end apart: 16 -> 17, of which waited for: 4 -> 5; matrix products, arithmetic and copies ran while one was open for 1% -> 1% of each run, Pallas kernels for 0% -> 0%
where the time goes in v1:
time: 245 us; the launch traced here: 244 us
  blocking collectives  94.9 us (39%)
  starting transfers between devices  67.1 us (27%)
  waiting for transfers between devices  38.5 us (16%)
  other arithmetic  27.5 us (11%)
  local copies, waits for them, and re-layouts  9.26 us (4%)
  matrix products  5.1 us (2%)
    psum x8, blocking collectives, over_axes(): return functools.reduce(lax.psum, axes, x)  94.9 us
    ppermute x16, starting transfers between devices, shifted(): lax.ppermute(value, axis, [(source, source + steps) for source in range(i...  41 us
    all_to_all x1, waiting for transfers between devices, per_device(): lax.all_to_all(jnp.stack([coarse_in] * lax.axis_size(GX_GY), axis=0), GX_...  33.6 us
    all_to_all x1, starting transfers between devices, per_device(): lax.all_to_all(jnp.stack([coarse_in] * lax.axis_size(GX_GY), axis=0), GX_...  26.1 us
    scatter-add x3, other arithmetic, place_parts(): empty.at[slot_table.reshape(-1)].add(signed_parts.reshape(-1, load_cases))  20.1 us
  transfers between devices with their start and end apart: 17, of which 5 were waited for; matrix products, arithmetic and copies ran while one was open for 1% of the time, Pallas kernels for 0%

profile of v1, /device:TPU:1, one launch (start us, length us, event | category | flops | bytes accessed | tf_op | source)
XLA Modules:
  0.0 244.0 jit_solution(17737646935898276196)
XLA Ops:
  2.7 4.6 %collective-permute-start.1 = (f32[192,128]{1,0:T(8,128)S(1)}, f32[192,128]{1,0:T(8,128)S(1)}, u32[]{:S(2)}, u32[]{:S(2)}) collective-permute-start(f32[192,128]{1,0:T(8,128)S(1)} %get-tuple-element.54), channel_id=1, source_target_pairs={{0,1},{1,2},{2,3},{3,4},{4,5},{5,6},{6,7},{7,8},{8,9},{9,10},{10,1... | collective-permute-start | bytes 294920 | tf_op jit(solution)/shard_map/ppermute | solution.py:17
  7.3 3.1 %collective-permute-start = (f32[192,128]{1,0:T(8,128)S(1)}, f32[192,128]{1,0:T(8,128)S(1)}, u32[]{:S(2)}, u32[]{:S(2)}) collective-permute-start(f32[192,128]{1,0:T(8,128)S(1)} %get-tuple-element.51), channel_id=1, source_target_pairs={{0,16},{16,32},{32,48},{48,64},{64,80},{80,96},{96,112},{112,128},... | collective-permute-start | bytes 294920 | tf_op jit(solution)/shard_map/ppermute | solution.py:17
  13.7 6.6 %scatter_custom_fusion = f32[768,128]{1,0:T(8,128)S(1)} fusion(s32[768]{0:T(1024)S(1)} %fusion.40, f32[768,128]{1,0:T(8,128)S(1)} %bitcast_multiply_fusion.2, f32[]{:T(128)} %constant.2.clone.1), kind=kCustom, calls=%fused_computation.53 | custom fusion | flops 98304 | bytes 393220 | tf_op jit(solution)/shard_map/scatter-add | solution.py:33
  22.9 3.0 %collective-permute-start.4 = (f32[192,128]{1,0:T(8,128)S(1)}, f32[192,128]{1,0:T(8,128)S(1)}, u32[]{:S(2)}, u32[]{:S(2)}) collective-permute-start(f32[192,128]{1,0:T(8,128)S(1)} %get-tuple-element.47), channel_id=1, source_target_pairs={{0,16},{16,32},{32,48},{48,64},{64,80},{80,96},{96,112},{112,128},... | collective-permute-start | bytes 294920 | tf_op jit(solution)/shard_map/ppermute | solution.py:17
  25.9 3.4 %collective-permute-start.5 = (f32[192,128]{1,0:T(8,128)S(1)}, f32[192,128]{1,0:T(8,128)S(1)}, u32[]{:S(2)}, u32[]{:S(2)}) collective-permute-start(f32[192,128]{1,0:T(8,128)S(1)} %get-tuple-element.49), channel_id=1, source_target_pairs={{0,1},{1,2},{2,3},{3,4},{4,5},{5,6},{6,7},{7,8},{8,9},{9,10},{10,1... | collective-permute-start | bytes 294920 | tf_op jit(solution)/shard_map/ppermute | solution.py:17
  30.6 2.5 %collective-permute-start.3 = (f32[192,128]{1,0:T(8,128)S(1)}, f32[192,128]{1,0:T(8,128)S(1)}, u32[]{:S(2)}, u32[]{:S(2)}) collective-permute-start(f32[192,128]{1,0:T(8,128)S(1)} %get-tuple-element.48), channel_id=1, source_target_pairs={{1,0},{2,1},{3,2},{4,3},{5,4},{6,5},{7,6},{8,7},{9,8},{10,9},{11,1... | collective-permute-start | bytes 294920 | tf_op jit(solution)/shard_map/ppermute | solution.py:17
  37.6 6.6 %scatter_custom_fusion.1 = f32[768,128]{1,0:T(8,128)S(1)} fusion(s32[768]{0:T(1024)S(1)} %fusion.40, f32[768,128]{1,0:T(8,128)S(1)} %bitcast_multiply_fusion.1, f32[]{:T(128)} %constant.2.clone.1), kind=kCustom, calls=%fused_computation.51 | custom fusion | flops 98304 | bytes 393220 | tf_op jit(solution)/shard_map/scatter-add | solution.py:33
  45.7 26.1 %all-to-all-start = ((f32[512,3,128]{2,1,0:T(4,128)}), f32[512,3,128]{2,1,0:T(4,128)S(1)}, u32[]{:S(2)}, u32[]{:S(2)}) async-start(f32[512,3,128]{2,1,0:T(4,128)} %stack.87), calls=%async_computation | async-start | bytes 2097152 | tf_op jit(solution)/shard_map/all_to_all | solution.py:125
  71.8 33.6 %all-to-all-done = f32[512,3,128]{2,1,0:T(4,128)S(1)} async-done(((f32[512,3,128]{2,1,0:T(4,128)}), f32[512,3,128]{2,1,0:T(4,128)S(1)}, u32[]{:S(2)}, u32[]{:S(2)}) %all-to-all-start) | async-done | bytes 786464 | tf_op jit(solution)/shard_map/all_to_all | solution.py:125
  113.2 3.1 %collective-permute-start.9 = (f32[192,128]{1,0:T(8,128)S(1)}, f32[192,128]{1,0:T(8,128)S(1)}, u32[]{:S(2)}, u32[]{:S(2)}) collective-permute-start(f32[192,128]{1,0:T(8,128)S(1)} %get-tuple-element.40), channel_id=1, source_target_pairs={{1,0},{2,1},{3,2},{4,3},{5,4},{6,5},{7,6},{8,7},{9,8},{10,9},{11,1... | collective-permute-start | bytes 294920 | tf_op jit(solution)/shard_map/ppermute | solution.py:17
  116.3 2.5 %collective-permute-start.8 = (f32[192,128]{1,0:T(8,128)S(1)}, f32[192,128]{1,0:T(8,128)S(1)}, u32[]{:S(2)}, u32[]{:S(2)}) collective-permute-start(f32[192,128]{1,0:T(8,128)S(1)} %get-tuple-element.41), channel_id=1, source_target_pairs={{0,1},{1,2},{2,3},{3,4},{4,5},{5,6},{6,7},{7,8},{8,9},{9,10},{10,1... | collective-permute-start | bytes 294920 | tf_op jit(solution)/shard_map/ppermute | solution.py:17
  118.8 2.2 collective-permute-start.11
  121.1 4.3 %collective-permute-start.10 = (f32[192,16]{0,1:T(8,128)S(1)}, f32[192,16]{0,1:T(8,128)S(1)}, u32[]{:S(2)}, u32[]{:S(2)}) collective-permute-start(f32[192,16]{0,1:T(8,128)S(1)} %get-tuple-element.55), channel_id=1, source_target_pairs={{0,16},{16,32},{32,48},{48,64},{64,80},{80,96},{96,112},{112,128},... | collective-permute-start | bytes 36872 | tf_op jit(solution)/shard_map/ppermute | solution.py:17
  126.0 13.8 %psum.88 = f32[16,128]{1,0:T(8,128)S(1)} all-reduce(f32[16,128]{1,0:T(8,128)S(1)} %fusion.10), channel_id=1, replica_groups=mesh['gx_0'=8,'gx_1'=4,'gy_0'=8,'gy_1'=2] {'gx_0'}, use_global_device_ids=true, to_apply=%region_7.9 | all-reduce | flops 2048 | bytes 16384 | tf_op jit(solution)/shard_map/psum | solution.py:21
  139.7 9.2 %psum.89 = f32[16,128]{1,0:T(8,128)S(1)} all-reduce(f32[16,128]{1,0:T(8,128)S(1)} %psum.88), channel_id=1, replica_groups=mesh['gx_0'=8,'gx_1'=4,'gy_0'=8,'gy_1'=2] {'gx_1'}, use_global_device_ids=true, to_apply=%region_8.10 | all-reduce | flops 2048 | bytes 16384 | tf_op jit(solution)/shard_map/psum | solution.py:21
  149.0 12.4 %psum.90 = f32[16,128]{1,0:T(8,128)S(1)} all-reduce(f32[16,128]{1,0:T(8,128)S(1)} %psum.89), channel_id=1, replica_groups=mesh['gx_0'=8,'gx_1'=4,'gy_0'=8,'gy_1'=2] {'gy_0'}, use_global_device_ids=true, to_apply=%region_9.11 | all-reduce | flops 2048 | bytes 16384 | tf_op jit(solution)/shard_map/psum | solution.py:21
  161.4 11.6 %psum.91 = f32[16,128]{1,0:T(8,128)S(1)} all-reduce(f32[16,128]{1,0:T(8,128)S(1)} %psum.90), channel_id=1, replica_groups=mesh['gx_0'=8,'gx_1'=4,'gy_0'=8,'gy_1'=2] {'gy_1'}, use_global_device_ids=true, to_apply=%region_10.12 | all-reduce | flops 2048 | bytes 16384 | tf_op jit(solution)/shard_map/psum | solution.py:21
  174.7 6.9 %scatter_custom_fusion.2 = f32[768,128]{1,0:T(8,128)S(1)} fusion(s32[768]{0:T(1024)} %copy-done.31, f32[768,128]{1,0:T(8,128)S(1)} %bitcast_multiply_fusion, f32[]{:T(128)} %constant.2.clone.1), kind=kCustom, calls=%fused_computation.49 | custom fusion | flops 98304 | bytes 393728 | tf_op jit(solution)/shard_map/scatter-add | solution.py:33
  187.0 2.4 collective-permute-start.13
  189.4 3.1 %collective-permute-start.15 = (f32[192,128]{1,0:T(8,128)S(1)}, f32[192,128]{1,0:T(8,128)S(1)}, u32[]{:S(2)}, u32[]{:S(2)}) collective-permute-start(f32[192,128]{1,0:T(8,128)S(1)} %get-tuple-element.23), channel_id=1, source_target_pairs={{0,1},{1,2},{2,3},{3,4},{4,5},{5,6},{6,7},{7,8},{8,9},{9,10},{10,1... | collective-permute-start | bytes 294920 | tf_op jit(solution)/shard_map/ppermute | solution.py:17
  194.5 16.3 %all-reduce.1 = (f32[128]{0:T(128)S(1)}, f32[128]{0:T(128)S(1)}) all-reduce(f32[128]{0:T(128)S(1)} %fusion.9, f32[128]{0:T(128)S(1)} %fusion.14), channel_id=1, replica_groups=mesh['gx_0'=8,'gx_1'=4,'gy_0'=8,'gy_1'=2] {'gx_0'}, use_global_device_ids=true, to_apply=%region_2.4 | all-reduce | flops 256 | bytes 2048 | tf_op jit(solution)/shard_map/psum | solution.py:21
  210.8 6.6 %all-reduce.2 = (f32[128]{0:T(128)S(1)}, f32[128]{0:T(128)S(1)}) all-reduce(f32[128]{0:T(128)S(1)} %get-tuple-element.5, f32[128]{0:T(128)S(1)} %get-tuple-element.6), channel_id=1, replica_groups=mesh['gx_0'=8,'gx_1'=4,'gy_0'=8,'gy_1'=2] {'gx_1'}, use_global_device_ids=true, to_apply=%region_3.5 | all-reduce | flops 256 | bytes 2048 | tf_op jit(solution)/shard_map/psum | solution.py:21
  217.3 11.5 %all-reduce = (f32[128]{0:T(128)S(1)}, f32[128]{0:T(128)S(1)}) all-reduce(f32[128]{0:T(128)S(1)} %get-tuple-element.7, f32[128]{0:T(128)S(1)} %get-tuple-element.8), channel_id=1, replica_groups=mesh['gx_0'=8,'gx_1'=4,'gy_0'=8,'gy_1'=2] {'gy_0'}, use_global_device_ids=true, to_apply=%region_4.6 | all-reduce | flops 256 | bytes 2048 | tf_op jit(solution)/shard_map/psum | solution.py:21
  228.9 13.6 %all-reduce.3 = (f32[128]{0:T(128)S(1)}, f32[128]{0:T(128)S(1)}) all-reduce(f32[128]{0:T(128)S(1)} %get-tuple-element.3, f32[128]{0:T(128)S(1)} %get-tuple-element.4), channel_id=1, replica_groups=mesh['gx_0'=8,'gx_1'=4,'gy_0'=8,'gy_1'=2] {'gy_1'}, use_global_device_ids=true, to_apply=%region_5.7 | all-reduce | flops 256 | bytes 2048 | tf_op jit(solution)/shard_map/psum | solution.py:21
  (142 shorter events, 33.4 us)
Async XLA Ops:
  1.5 35.1 %copy-start.19 = (f32[1,192]{1,0:T(1,128)}, f32[1,192]{1,0:T(1,128)S(1)}, u32[]{:S(2)}) copy-start(f32[1,192]{1,0:T(1,128)S(1)} %get-tuple-element.62) | copy-start | bytes 2308
  1.6 124.2 %copy-start.15 = (f32[384]{0:T(512)}, f32[384]{0:T(512)S(1)}, u32[]{:S(2)}) copy-start(f32[384]{0:T(512)S(1)} %pad_maximum_fusion.9) | copy-start | bytes 4612
  2.7 10.1 %collective-permute-start.1 = (f32[192,128]{1,0:T(8,128)S(1)}, f32[192,128]{1,0:T(8,128)S(1)}, u32[]{:S(2)}, u32[]{:S(2)}) collective-permute-start(f32[192,128]{1,0:T(8,128)S(1)} %get-tuple-element.54), channel_id=1, source_target_pairs={{0,1},{1,2},{2,3},{3,4},{4,5},{5,6},{6,7},{7,8},{8,9},{9,10},{10,1... | collective-permute-start | bytes 294920 | tf_op jit(solution)/shard_map/ppermute | solution.py:17
  7.3 5.6 %collective-permute-start = (f32[192,128]{1,0:T(8,128)S(1)}, f32[192,128]{1,0:T(8,128)S(1)}, u32[]{:S(2)}, u32[]{:S(2)}) collective-permute-start(f32[192,128]{1,0:T(8,128)S(1)} %get-tuple-element.51), channel_id=1, source_target_pairs={{0,16},{16,32},{32,48},{48,64},{64,80},{80,96},{96,112},{112,128},... | collective-permute-start | bytes 294920 | tf_op jit(solution)/shard_map/ppermute | solution.py:17
  12.8 95.7 %copy-start.13 = (s32[1024]{0:T(1024)}, s32[1024]{0:T(1024)S(1)}, u32[]{:S(2)}) copy-start(s32[1024]{0:T(1024)S(1)} %pad_clamp_fusion) | copy-start | bytes 12292
  22.9 10.2 %collective-permute-start.4 = (f32[192,128]{1,0:T(8,128)S(1)}, f32[192,128]{1,0:T(8,128)S(1)}, u32[]{:S(2)}, u32[]{:S(2)}) collective-permute-start(f32[192,128]{1,0:T(8,128)S(1)} %get-tuple-element.47), channel_id=1, source_target_pairs={{0,16},{16,32},{32,48},{48,64},{64,80},{80,96},{96,112},{112,128},... | collective-permute-start | bytes 294920 | tf_op jit(solution)/shard_map/ppermute | solution.py:17
  25.9 7.3 %collective-permute-start.5 = (f32[192,128]{1,0:T(8,128)S(1)}, f32[192,128]{1,0:T(8,128)S(1)}, u32[]{:S(2)}, u32[]{:S(2)}) collective-permute-start(f32[192,128]{1,0:T(8,128)S(1)} %get-tuple-element.49), channel_id=1, source_target_pairs={{0,1},{1,2},{2,3},{3,4},{4,5},{5,6},{6,7},{7,8},{8,9},{9,10},{10,1... | collective-permute-start | bytes 294920 | tf_op jit(solution)/shard_map/ppermute | solution.py:17
  29.3 5.4 %collective-permute-start.2 = (f32[192,128]{1,0:T(8,128)S(1)}, f32[192,128]{1,0:T(8,128)S(1)}, u32[]{:S(2)}, u32[]{:S(2)}) collective-permute-start(f32[192,128]{1,0:T(8,128)S(1)} %get-tuple-element.50), channel_id=1, source_target_pairs={{16,0},{32,16},{48,32},{64,48},{80,64},{96,80},{112,96},{128,112},... | collective-permute-start | bytes 294920 | tf_op jit(solution)/shard_map/ppermute | solution.py:17
  30.6 5.9 %collective-permute-start.3 = (f32[192,128]{1,0:T(8,128)S(1)}, f32[192,128]{1,0:T(8,128)S(1)}, u32[]{:S(2)}, u32[]{:S(2)}) collective-permute-start(f32[192,128]{1,0:T(8,128)S(1)} %get-tuple-element.48), channel_id=1, source_target_pairs={{1,0},{2,1},{3,2},{4,3},{5,4},{6,5},{7,6},{8,7},{9,8},{10,9},{11,1... | collective-permute-start | bytes 294920 | tf_op jit(solution)/shard_map/ppermute | solution.py:17
  45.7 59.7 %all-to-all-start = ((f32[512,3,128]{2,1,0:T(4,128)}), f32[512,3,128]{2,1,0:T(4,128)S(1)}, u32[]{:S(2)}, u32[]{:S(2)}) async-start(f32[512,3,128]{2,1,0:T(4,128)} %stack.87), calls=%async_computation | async-start | bytes 2097152 | tf_op jit(solution)/shard_map/all_to_all | solution.py:125
  110.4 10.7 %collective-permute-start.6 = (f32[192,128]{1,0:T(8,128)S(1)}, f32[192,128]{1,0:T(8,128)S(1)}, u32[]{:S(2)}, u32[]{:S(2)}) collective-permute-start(f32[192,128]{1,0:T(8,128)S(1)} %get-tuple-element.39), channel_id=1, source_target_pairs={{0,16},{16,32},{32,48},{48,64},{64,80},{80,96},{96,112},{112,128},... | collective-permute-start | bytes 294920 | tf_op jit(solution)/shard_map/ppermute | solution.py:17
  111.9 13.5 %collective-permute-start.7 = (f32[192,128]{1,0:T(8,128)S(1)}, f32[192,128]{1,0:T(8,128)S(1)}, u32[]{:S(2)}, u32[]{:S(2)}) collective-permute-start(f32[192,128]{1,0:T(8,128)S(1)} %get-tuple-element.42), channel_id=1, source_target_pairs={{16,0},{32,16},{48,32},{64,48},{80,64},{96,80},{112,96},{128,112},... | collective-permute-start | bytes 294920 | tf_op jit(solution)/shard_map/ppermute | solution.py:17
  113.2 12.2 %collective-permute-start.9 = (f32[192,128]{1,0:T(8,128)S(1)}, f32[192,128]{1,0:T(8,128)S(1)}, u32[]{:S(2)}, u32[]{:S(2)}) collective-permute-start(f32[192,128]{1,0:T(8,128)S(1)} %get-tuple-element.40), channel_id=1, source_target_pairs={{1,0},{2,1},{3,2},{4,3},{5,4},{6,5},{7,6},{8,7},{9,8},{10,9},{11,1... | collective-permute-start | bytes 294920 | tf_op jit(solution)/shard_map/ppermute | solution.py:17
  116.3 9.1 %collective-permute-start.8 = (f32[192,128]{1,0:T(8,128)S(1)}, f32[192,128]{1,0:T(8,128)S(1)}, u32[]{:S(2)}, u32[]{:S(2)}) collective-permute-start(f32[192,128]{1,0:T(8,128)S(1)} %get-tuple-element.41), channel_id=1, source_target_pairs={{0,1},{1,2},{2,3},{3,4},{4,5},{5,6},{6,7},{7,8},{8,9},{9,10},{10,1... | collective-permute-start | bytes 294920 | tf_op jit(solution)/shard_map/ppermute | solution.py:17
  118.8 54.1 %collective-permute-start.11 = (f32[192,16]{0,1:T(8,128)S(1)}, f32[192,16]{0,1:T(8,128)S(1)}, u32[]{:S(2)}, u32[]{:S(2)}) collective-permute-start(f32[192,16]{0,1:T(8,128)S(1)} %get-tuple-element.58), channel_id=1, source_target_pairs={{0,1},{1,2},{2,3},{3,4},{4,5},{5,6},{6,7},{7,8},{8,9},{9,10},{10,1... | collective-permute-start | bytes 36872 | tf_op jit(solution)/shard_map/ppermute | solution.py:17
  121.1 51.8 %collective-permute-start.10 = (f32[192,16]{0,1:T(8,128)S(1)}, f32[192,16]{0,1:T(8,128)S(1)}, u32[]{:S(2)}, u32[]{:S(2)}) collective-permute-start(f32[192,16]{0,1:T(8,128)S(1)} %get-tuple-element.55), channel_id=1, source_target_pairs={{0,16},{16,32},{32,48},{48,64},{64,80},{80,96},{96,112},{112,128},... | collective-permute-start | bytes 36872 | tf_op jit(solution)/shard_map/ppermute | solution.py:17
  184.2 58.3 %copy-start.4 = (f32[192,128]{1,0:T(8,128)S(1)}, f32[192,128]{1,0:T(8,128)}, u32[]{:S(2)}) copy-start(f32[192,128]{1,0:T(8,128)} %copy-done.3) | copy-start | bytes 294916
  184.2 58.2 %copy-start.6 = (f32[192,128]{1,0:T(8,128)S(1)}, f32[192,128]{1,0:T(8,128)}, u32[]{:S(2)}) copy-start(f32[192,128]{1,0:T(8,128)} %copy-done.5) | copy-start | bytes 294916
  184.3 8.5 %collective-permute-start.14 = (f32[192,128]{1,0:T(8,128)S(1)}, f32[192,128]{1,0:T(8,128)S(1)}, u32[]{:S(2)}, u32[]{:S(2)}) collective-permute-start(f32[192,128]{1,0:T(8,128)S(1)} %get-tuple-element.21), channel_id=1, source_target_pairs={{0,16},{16,32},{32,48},{48,64},{64,80},{80,96},{96,112},{112,128},... | collective-permute-start | bytes 294920 | tf_op jit(solution)/shard_map/ppermute | solution.py:17
  185.7 7.0 %collective-permute-start.12 = (f32[192,128]{1,0:T(8,128)S(1)}, f32[192,128]{1,0:T(8,128)S(1)}, u32[]{:S(2)}, u32[]{:S(2)}) collective-permute-start(f32[192,128]{1,0:T(8,128)S(1)} %get-tuple-element.24), channel_id=1, source_target_pairs={{16,0},{32,16},{48,32},{64,48},{80,64},{96,80},{112,96},{128,112},... | collective-permute-start | bytes 294920 | tf_op jit(solution)/shard_map/ppermute | solution.py:17
  187.0 5.9 %collective-permute-start.13 = (f32[192,128]{1,0:T(8,128)S(1)}, f32[192,128]{1,0:T(8,128)S(1)}, u32[]{:S(2)}, u32[]{:S(2)}) collective-permute-start(f32[192,128]{1,0:T(8,128)S(1)} %get-tuple-element.22), channel_id=1, source_target_pairs={{1,0},{2,1},{3,2},{4,3},{5,4},{6,5},{7,6},{8,7},{9,8},{10,9},{11,1... | collective-permute-start | bytes 294920 | tf_op jit(solution)/shard_map/ppermute | solution.py:17
  189.4 4.8 %collective-permute-start.15 = (f32[192,128]{1,0:T(8,128)S(1)}, f32[192,128]{1,0:T(8,128)S(1)}, u32[]{:S(2)}, u32[]{:S(2)}) collective-permute-start(f32[192,128]{1,0:T(8,128)S(1)} %get-tuple-element.23), channel_id=1, source_target_pairs={{0,1},{1,2},{2,3},{3,4},{4,5},{5,6},{6,7},{7,8},{8,9},{9,10},{10,1... | collective-permute-start | bytes 294920 | tf_op jit(solution)/shard_map/ppermute | solution.py:17
  194.4 48.2 %copy-start.7 = (f32[1,1,192,128]{3,2,1,0:T(8,128)S(1)}, f32[1,1,192,128]{3,2,1,0:T(8,128)}, u32[]{:S(2)}) copy-start(f32[1,1,192,128]{3,2,1,0:T(8,128)} %get-tuple-element.27) | copy-start | bytes 294916
  194.4 48.2 %copy-start.8 = (f32[1,1,192,128]{3,2,1,0:T(8,128)S(1)}, f32[1,1,192,128]{3,2,1,0:T(8,128)}, u32[]{:S(2)}) copy-start(f32[1,1,192,128]{3,2,1,0:T(8,128)} %get-tuple-element.29) | copy-start | bytes 294916
  (25 other events, 344.0 us)
